TPU v7x, 32 devices: a whole 2x2x4 slice. The times are simulated.
32 devices in a mesh: groups: 2 (over x), pts: 8 (over z, y), lm: 2 (over core).
Axes of the slice: x: 2, y: 2, z: 4, core: 2. Of those that a mesh axis runs over, the one named last changes fastest.
Arguments:
- points: float32 [3, 4096], P(None, ('groups', 'pts', 'lm')), parts along dimension 1, may hold values from 0 to 1, as said below
- targets: float32 [32, 4096], P(None, ('groups', 'pts', 'lm')), parts along dimension 1, may hold values from -12 to 12
- order: int32 [4096], P(('groups', 'pts', 'lm')), parts along dimension 0, may hold values from 0 to 2047, as said below
- landmarks: int32 [2048], P('groups'), parts along dimension 0, may hold values from 0 to 2047, as said below
Outputs:
- coefficients: float32 [32, 4096], P(None, ('groups', 'pts', 'lm')), parts along dimension 1
- residual: float32 [32, 4096], P(None, ('groups', 'pts', 'lm')), parts along dimension 1
There are 2 independent parts, one for each index of `groups`. A program takes and returns all parts, laid end to end along the dimension named above; each array names one. Nothing has to cross between parts.
Inputs may be any that keep to these rules, and one draw needn't show every extreme that they name: Each column is a point of the unit cube. Points are stored in Z-order: the 128 points of each aligned block of columns lie in one box of a regular grid, and consecutive blocks follow the Z-order curve through the boxes. `order`: A permutation of 0 to 2047. `landmarks`: 1024 distinct point indices.
All inputs are finite; a program needn't handle non-finite values.
Results may differ from a plain program's by a relative error of at most 0.0003.
Values sent between devices are 32-bit elements; how exact they have to be, the bound alone decides.
No kernel may reach another device: no remote copies, remote signals or barrier semaphores. Data moves between devices by JAX's collectives and lax.ppermute only.
A program may use at most 128 MiB of HBM per device.

v0:
```python
import math
import jax
import jax.numpy as jnp
from jax import lax
from jax.sharding import PartitionSpec as P

ITERS = 2
root_five = 2.23606797749979
signal_var = 0.1
inverse_square_length = 25.0
highest = lax.Precision.HIGHEST


def matern(near, far):
    first = near[0][:, None] - far[0][None, :]
    second = near[1][:, None] - far[1][None, :]
    third = near[2][:, None] - far[2][None, :]
    scaled = (first * first + second * second + third * third) * inverse_square_length
    reach = jnp.sqrt(scaled)
    return signal_var * (1.0 + root_five * reach + 5.0 / 3.0 * scaled) * jnp.exp(-root_five * reach)


def tile_product(near, piece):
    width = piece.shape[1]
    block = math.gcd(width, 512)

    def accumulate(index, total):
        slab = lax.dynamic_slice_in_dim(piece, index * block, block, 1)
        return total + jnp.dot(slab[3:], matern(slab[:3], near), precision=highest)

    empty = jnp.zeros((piece.shape[0] - 3, near.shape[1]), jnp.float32)
    return lax.fori_loop(0, width // block, accumulate, empty)


def landmark_total(vector, cross):
    return lax.psum(jnp.dot(vector, cross, precision=highest), ("pts", "lm"))


def body(points, targets, order, landmarks):
    rows = points.shape[1]
    count = landmarks.shape[0]
    offset = lax.axis_index(("pts", "lm")) * rows
    every = lax.all_gather(targets, ("pts", "lm"), axis=1, tiled=True)
    goal = jnp.take(every, order, axis=1)
    local = landmarks - offset
    inside = (local >= 0) & (local < rows)
    picked = jnp.where(inside[None, :], jnp.take(points, jnp.clip(local, 0, rows - 1), axis=1), 0.0)
    anchors = lax.psum(picked, ("pts", "lm"))
    cross = matern(points, anchors)
    gram = lax.psum(jnp.einsum("ri,rj->ij", cross, cross, precision=highest), ("pts", "lm"))
    inner = matern(anchors, anchors) + jnp.eye(count, dtype=jnp.float32) + gram
    factor = jnp.linalg.cholesky(inner)
    solution = jnp.zeros_like(goal)
    residual = goal
    summed = landmark_total(residual, cross)
    for step in range(ITERS):
        weights = jax.scipy.linalg.cho_solve((factor, True), summed.T)
        scaled_res = residual - jnp.dot(cross, weights, precision=highest).T
        stacked = jnp.concatenate([points, scaled_res], axis=0)
        image = (
            tile_product(points, lax.all_gather(stacked, ("pts", "lm"), axis=1, tiled=True))
            + scaled_res
        )
        current, curvature, lifted = lax.psum(
            (
                jnp.sum(residual * scaled_res, axis=1),
                jnp.sum(scaled_res * image, axis=1),
                jnp.dot(image, cross, precision=highest),
            ),
            ("pts", "lm"),
        )
        if step == 0:
            stride = current / curvature
            direction = scaled_res
            along = image
            along_lift = lifted
        else:
            ratio = current / previous
            stride = current / (curvature - ratio * current / stride)
            direction = scaled_res + ratio[:, None] * direction
            along = image + ratio[:, None] * along
            along_lift = lifted + ratio[:, None] * along_lift
        solution = solution + stride[:, None] * direction
        residual = residual - stride[:, None] * along
        summed = summed - stride[:, None] * along_lift
        previous = current
    return (solution, residual)


def solution(mesh):
    return jax.shard_map(
        body,
        mesh=mesh,
        in_specs=(
            P(None, ("groups", "pts", "lm")),
            P(None, ("groups", "pts", "lm")),
            P(("groups", "pts", "lm")),
            P("groups"),
        ),
        out_specs=(P(None, ("groups", "pts", "lm")), P(None, ("groups", "pts", "lm"))),
        check_vma=False,
    )
```

profile of v0, /device:TPU:0, one launch (start us, length us, event | category | flops | bytes accessed | tf_op | source)
XLA Modules:
  0.0 779.8 jit_solution(6662976577567026140)
XLA Ops:
  11.5 2.8 gather_fusion.1
  14.7 68.3 %psum.56 = f32[3,1024]{0,1:T(8,128)S(1)} all-reduce(f32[3,1024]{0,1:T(8,128)S(1)} %select_bitcast_fusion), channel_id=1, replica_groups=mesh['groups'=2,'pts'=8,'lm'=2] {'pts','lm'}, use_global_device_ids=true, to_apply=%region_0.1 | all-reduce | flops 3072 | bytes 24576 | tf_op jit(solution)/shard_map/psum | solution.py:48
  84.6 21.3 %all_gather.9 = f32[32,2048]{0,1:T(8,128)S(1)} all-gather(f32[32,128]{0,1:T(8,128)S(1)} %copy.11), channel_id=1, replica_groups=mesh['groups'=2,'pts'=8,'lm'=2] {'pts','lm'}, dimensions={1}, use_global_device_ids=true | all-gather | bytes 278528 | tf_op jit(solution)/shard_map/all_gather | solution.py:43
  106.6 6.6 fusion.103
  114.9 112.6 %all-reduce.9.cloned.1.call-done = (f32[1024,1024]{0,1:T(8,128)}, f32[32,1024]{1,0:T(8,128)}) async-done(((f32[1024,1024]{0,1:T(8,128)}, f32[32,1024]{1,0:T(8,128)}), (f32[1024,1024]{0,1:T(8,128)}, f32[32,1024]{1,0:T(8,128)})) %all-reduce.9.cloned.1.call-update) | async-done | bytes 4325392 | tf_op jit(solution)/shard_map/psum | solution.py:50
  227.5 7.6 add_add_fusion
  235.1 5.3 copy.15
  240.5 7.4 fusion.74
  249.8 11.7 %cholesky.223 = f32[128,128]{1,0:T(8,128)S(1)} custom-call(f32[128,128]{1,0:T(8,128)S(1)} %cholesky.580), custom_call_target="Cholesky" | custom-call | tf_op jit(solution)/shard_map/jit(cholesky)/cholesky | solution.py:52
  261.5 2.5 cholesky.255
  264.0 9.8 %custom-call.64 = f32[1,128,128]{1,2,0:T(8,128)S(1)} custom-call(f32[1,128,128]{2,1,0:T(8,128)S(1)} %get-tuple-element.346), custom_call_target="InvertDiagBlocksLowerTriangular" | custom-call | tf_op jit(solution)/shard_map/jit(cholesky)/cholesky | solution.py:52
  273.8 2.4 constant_dynamic-update-slice_fusion.93
  277.8 11.7 %cholesky.244 = f32[128,128]{1,0:T(8,128)S(1)} custom-call(f32[128,128]{1,0:T(8,128)S(1)} %cholesky.584), custom_call_target="Cholesky" | custom-call | tf_op jit(solution)/shard_map/jit(cholesky)/cholesky | solution.py:52
  290.1 10.0 %custom-call.65 = f32[1,128,128]{1,2,0:T(8,128)S(1)} custom-call(f32[1,128,128]{2,1,0:T(8,128)S(1)} %get-tuple-element.343), custom_call_target="InvertDiagBlocksLowerTriangular" | custom-call | tf_op jit(solution)/shard_map/jit(cholesky)/cholesky | solution.py:52
  301.4 2.1 convolution_subtract_fusion.1
  303.5 11.7 %cholesky.468 = f32[128,128]{1,0:T(8,128)S(1)} custom-call(f32[128,128]{1,0:T(8,128)S(1)} %cholesky.589), custom_call_target="Cholesky" | custom-call | tf_op jit(solution)/shard_map/jit(cholesky)/cholesky | solution.py:52
  316.4 9.8 %custom-call.66 = f32[1,128,128]{1,2,0:T(8,128)S(1)} custom-call(f32[1,128,128]{2,1,0:T(8,128)S(1)} %get-tuple-element.340), custom_call_target="InvertDiagBlocksLowerTriangular" | custom-call | tf_op jit(solution)/shard_map/jit(cholesky)/cholesky | solution.py:52
  327.4 2.3 convolution_subtract_fusion.2
  329.8 12.1 %cholesky.487 = f32[128,128]{1,0:T(8,128)S(1)} custom-call(f32[128,128]{1,0:T(8,128)S(1)} %cholesky.594), custom_call_target="Cholesky" | custom-call | tf_op jit(solution)/shard_map/jit(cholesky)/cholesky | solution.py:52
  343.2 9.8 %custom-call.67 = f32[1,128,128]{1,2,0:T(8,128)S(1)} custom-call(f32[1,128,128]{2,1,0:T(8,128)S(1)} %get-tuple-element.337), custom_call_target="InvertDiagBlocksLowerTriangular" | custom-call | tf_op jit(solution)/shard_map/jit(cholesky)/cholesky | solution.py:52
  354.1 2.3 convolution_subtract_fusion.3
  356.4 11.7 %cholesky.506 = f32[128,128]{1,0:T(8,128)S(1)} custom-call(f32[128,128]{1,0:T(8,128)S(1)} %cholesky.599), custom_call_target="Cholesky" | custom-call | tf_op jit(solution)/shard_map/jit(cholesky)/cholesky | solution.py:52
  369.4 9.8 %custom-call.68 = f32[1,128,128]{1,2,0:T(8,128)S(1)} custom-call(f32[1,128,128]{2,1,0:T(8,128)S(1)} %get-tuple-element.334), custom_call_target="InvertDiagBlocksLowerTriangular" | custom-call | tf_op jit(solution)/shard_map/jit(cholesky)/cholesky | solution.py:52
  380.3 2.5 convolution_subtract_fusion.4
  382.8 11.7 %cholesky.526 = f32[128,128]{1,0:T(8,128)S(1)} custom-call(f32[128,128]{1,0:T(8,128)S(1)} %cholesky.604), custom_call_target="Cholesky" | custom-call | tf_op jit(solution)/shard_map/jit(cholesky)/cholesky | solution.py:52
  395.7 9.8 %custom-call.69 = f32[1,128,128]{1,2,0:T(8,128)S(1)} custom-call(f32[1,128,128]{2,1,0:T(8,128)S(1)} %get-tuple-element.331), custom_call_target="InvertDiagBlocksLowerTriangular" | custom-call | tf_op jit(solution)/shard_map/jit(cholesky)/cholesky | solution.py:52
  406.5 2.0 convolution_subtract_fusion.5
  408.5 11.7 %cholesky.546 = f32[128,128]{1,0:T(8,128)S(1)} custom-call(f32[128,128]{1,0:T(8,128)S(1)} %cholesky.609), custom_call_target="Cholesky" | custom-call | tf_op jit(solution)/shard_map/jit(cholesky)/cholesky | solution.py:52
  421.5 10.0 %custom-call.70 = f32[1,128,128]{1,2,0:T(8,128)S(1)} custom-call(f32[1,128,128]{2,1,0:T(8,128)S(1)} %get-tuple-element.328), custom_call_target="InvertDiagBlocksLowerTriangular" | custom-call | tf_op jit(solution)/shard_map/jit(cholesky)/cholesky | solution.py:52
  434.1 11.7 %cholesky.564 = f32[128,128]{1,0:T(8,128)S(1)} custom-call(f32[128,128]{1,0:T(8,128)S(1)} %convolution_subtract_fusion.6), custom_call_target="Cholesky" | custom-call | tf_op jit(solution)/shard_map/jit(cholesky)/cholesky | solution.py:52
  452.8 4.8 select_select_fusion
  457.6 23.0 %while.38 = (s32[]{:T(128)}, f32[1024,1024]{1,0:T(8,128)}, s32[8,2]{0,1:T(2,128)S(1)}, f32[8,128,128]{2,1,0:T(8,128)S(1)}, s32[]{:T(128)}) while((s32[]{:T(128)}, f32[1024,1024]{1,0:T(8,128)}, s32[8,2]{0,1:T(2,128)S(1)}, f32[8,128,128]{2,1,0:T(8,128)S(1)}, s32[]{:T(128)}) %tuple.182), condition=%wide.while_cond, body=%wide.while_body.sunk | while | flops 2 | bytes 131181 | solution.py:57
  458.2 2.3 bitcast_dynamic-update-slice_fusion.2
  461.1 2.3 bitcast_dynamic-update-slice_fusion.2
  464.0 2.3 bitcast_dynamic-update-slice_fusion.2
  466.8 2.3 bitcast_dynamic-update-slice_fusion.2
  469.7 2.3 bitcast_dynamic-update-slice_fusion.2
  472.6 2.3 bitcast_dynamic-update-slice_fusion.2
  475.5 2.3 bitcast_dynamic-update-slice_fusion.2
  478.4 2.2 bitcast_dynamic-update-slice_fusion.2
  480.6 78.8 %custom-call.74 = f32[8,128,128]{1,2,0:T(8,128)S(1)} custom-call(f32[8,128,128]{2,1,0:T(8,128)S(1)} %get-tuple-element.269), custom_call_target="InvertDiagBlocksLowerTriangular" | custom-call | tf_op jit(solution)/shard_map/jit(_cho_solve)/triangular_solve | solution.py:57
  582.0 20.4 %all_gather.10 = f32[35,2048]{1,0:T(8,128)S(1)} all-gather(f32[35,128]{1,0:T(8,128)S(1)} %pad_maximum_fusion.1), channel_id=1, replica_groups=mesh['groups'=2,'pts'=8,'lm'=2] {'pts','lm'}, dimensions={1}, use_global_device_ids=true | all-gather | bytes 304640 | tf_op jit(solution)/shard_map/all_gather | solution.py:61
  602.5 2.7 while.36
  606.9 30.1 %all-reduce.2 = (f32[32]{0:T(128)S(1)}, f32[32]{0:T(128)S(1)}) all-reduce(f32[32]{0:T(128)S(1)} %get-tuple-element.277, f32[32]{0:T(128)S(1)} %get-tuple-element.276), channel_id=1, replica_groups=mesh['groups'=2,'pts'=8,'lm'=2] {'pts','lm'}, use_global_device_ids=true, to_apply=%region_20.22 | all-reduce | flops 64 | bytes 512 | tf_op jit(solution)/shard_map/psum | solution.py:64
  637.0 55.5 %all-reduce.7.cloned.1.call-done = f32[32,1024]{1,0:T(8,128)} async-done(((f32[32,1024]{1,0:T(8,128)}), f32[32,1024]{1,0:T(8,128)}) %all-reduce.7.cloned.1.call-update) | async-done | bytes 131088 | tf_op jit(solution)/shard_map/psum | solution.py:64
  716.1 22.9 %all_gather.11 = f32[35,2048]{1,0:T(8,128)S(1)} all-gather(f32[35,128]{1,0:T(8,128)S(1)} %pad_maximum_fusion), channel_id=1, replica_groups=mesh['groups'=2,'pts'=8,'lm'=2] {'pts','lm'}, dimensions={1}, use_global_device_ids=true | all-gather | bytes 304640 | tf_op jit(solution)/shard_map/all_gather | solution.py:61
  739.0 2.7 while.37
  741.9 29.8 %all-reduce.1 = (f32[32]{0:T(128)S(1)}, f32[32]{0:T(128)S(1)}) all-reduce(f32[32]{0:T(128)S(1)} %get-tuple-element.275, f32[32]{0:T(128)S(1)} %get-tuple-element.274), channel_id=1, replica_groups=mesh['groups'=2,'pts'=8,'lm'=2] {'pts','lm'}, use_global_device_ids=true, to_apply=%region_27.29 | all-reduce | flops 64 | bytes 512 | tf_op jit(solution)/shard_map/psum | solution.py:64
  (213 shorter events, 87.2 us)
Async XLA Ops:
  7.2 220.3 %all-reduce.9.cloned.1.call-start = ((), (), s32[]{:S(2)}) async-start(), calls=%async_computation.1 | async-start | bytes 8650752 | tf_op jit(solution)/shard_map/psum | solution.py:50
  114.9 577.7 %all-reduce.7.cloned.1.call-start = ((), (), s32[]{:S(2)}) async-start(), calls=%async_computation | async-start | bytes 262144 | tf_op jit(solution)/shard_map/psum | solution.py:64
  247.8 1.9 copy-start
  452.8 106.7 %copy-start.1 = (f32[32,1024]{1,0:T(8,128)S(1)}, f32[32,1024]{1,0:T(8,128)}, u32[]{:S(2)}) copy-start(f32[32,1024]{1,0:T(8,128)} %get-tuple-element.307) | copy-start | bytes 393220
  565.1 16.9 %copy-start.2 = (f32[3,128]{1,0:T(4,128)S(1)}, f32[3,128]{1,0:T(4,128)}, u32[]{:S(2)}) copy-start(f32[3,128]{1,0:T(4,128)} %param.10) | copy-start | bytes 4612
Sparse Core Ops, SparseCore 0:
  115.0 112.4 all-reduce.8
  607.0 85.4 all-reduce.6
where the time goes:
time: 789 us; the launch traced here: 780 us
  other arithmetic  276 us (35%)
  blocking collectives  193 us (24%)
  waiting for transfers between devices  168 us (21%)
  matrix products  81.6 us (10%)
  local copies, waits for them, and re-layouts  40.4 us (5%)
  between operations  20.6 us (3%)
    another operation x30, other arithmetic, body(): factor = jnp.linalg.cholesky(inner)  172 us
    psum x1, waiting for transfers between devices, body(): lax.psum(jnp.einsum('ri,rj->ij', cross, cross, precision=highest), ('pts'...  113 us
    another operation x4, other arithmetic, body(): weights = jax.scipy.linalg.cho_solve((factor, True), summed.T)  83.7 us
    psum x1, blocking collectives, body(): anchors = lax.psum(picked, ('pts', 'lm'))  68.3 us
    psum x2, blocking collectives, body(): lax.psum((jnp.sum(residual * scaled_res, axis=1), jnp.sum(scaled_res * im...  59.9 us
    psum x1, waiting for transfers between devices, body(): lax.psum((jnp.sum(residual * scaled_res, axis=1), jnp.sum(scaled_res * im...  55.5 us
    all_gather x2, blocking collectives, body(): lax.all_gather(stacked, ('pts', 'lm'), axis=1, tiled=True)  43.3 us
    another operation x60, matrix products, body(): weights = jax.scipy.linalg.cho_solve((factor, True), summed.T)  41.8 us
  transfers between devices with their start and end apart: 2, of which 2 were waited for; matrix products, arithmetic and copies ran while one was open for 0% of the time, Pallas kernels for 0%

commit v1 on v0

--- a/solution.py
+++ b/solution.py
@@ -45,7 +45,8 @@
     local = landmarks - offset
     inside = (local >= 0) & (local < rows)
     picked = jnp.where(inside[None, :], jnp.take(points, jnp.clip(local, 0, rows - 1), axis=1), 0.0)
-    anchors = lax.psum(picked, ("pts", "lm"))
+    parts = lax.all_gather(picked, ("pts", "lm"))
+    anchors = jnp.sum(parts, axis=0)
     cross = matern(points, anchors)
     gram = lax.psum(jnp.einsum("ri,rj->ij", cross, cross, precision=highest), ("pts", "lm"))
     inner = matern(anchors, anchors) + jnp.eye(count, dtype=jnp.float32) + gram

time: 789 us -> 742 us (0.940)
  blocking collectives: 193 us -> 148 us
    psum x1 -> x0, blocking collectives: 68.3 us -> none  [body(): anchors = lax.psum(picked, ('pts', 'lm'))]
    all_gather x0 -> x1, blocking collectives: none -> 23.8 us  [body(): parts = lax.all_gather(picked, ('pts', 'lm'))]
where the time goes in v1:
time: 742 us; the launch traced here: 733 us
  other arithmetic  276 us (37%)
  waiting for transfers between devices  167 us (23%)
  blocking collectives  148 us (20%)
  matrix products  81.2 us (11%)
  local copies, waits for them, and re-layouts  39.8 us (5%)
  between operations  20.6 us (3%)
    another operation x30, other arithmetic, body(): factor = jnp.linalg.cholesky(inner)  172 us
    psum x1, waiting for transfers between devices, body(): lax.psum(jnp.einsum('ri,rj->ij', cross, cross, precision=highest), ('pts'...  112 us
    another operation x4, other arithmetic, body(): weights = jax.scipy.linalg.cho_solve((factor, True), summed.T)  83.7 us
    psum x2, blocking collectives, body(): lax.psum((jnp.sum(residual * scaled_res, axis=1), jnp.sum(scaled_res * im...  59.9 us
    psum x1, waiting for transfers between devices, body(): lax.psum((jnp.sum(residual * scaled_res, axis=1), jnp.sum(scaled_res * im...  55.5 us
    all_gather x2, blocking collectives, body(): lax.all_gather(stacked, ('pts', 'lm'), axis=1, tiled=True)  43.3 us
    another operation x60, matrix products, body(): weights = jax.scipy.linalg.cho_solve((factor, True), summed.T)  41.4 us
    all_gather x1, blocking collectives, body(): parts = lax.all_gather(picked, ('pts', 'lm'))  23.8 us
  transfers between devices with their start and end apart: 2, of which 2 were waited for; matrix products, arithmetic and copies ran while one was open for 0% of the time, Pallas kernels for 0%

profile of v1, /device:TPU:0, one launch (start us, length us, event | category | flops | bytes accessed | tf_op | source)
XLA Modules:
  0.0 732.8 jit_solution(5149334190683457857)
XLA Ops:
  11.5 2.8 gather_fusion.1
  14.9 23.8 %all_gather.14 = f32[16,3,1024]{2,1,0:T(4,128)S(1)} all-gather(f32[1,3,1024]{2,1,0:T(4,128)S(1)} %copy.21), channel_id=1, replica_groups=mesh['groups'=2,'pts'=8,'lm'=2] {'pts','lm'}, dimensions={0}, use_global_device_ids=true | all-gather | bytes 208896 | tf_op jit(solution)/shard_map/all_gather | solution.py:48
  39.6 20.5 %all_gather.13 = f32[32,2048]{0,1:T(8,128)S(1)} all-gather(f32[32,128]{0,1:T(8,128)S(1)} %copy.18), channel_id=1, replica_groups=mesh['groups'=2,'pts'=8,'lm'=2] {'pts','lm'}, dimensions={1}, use_global_device_ids=true | all-gather | bytes 278528 | tf_op jit(solution)/shard_map/all_gather | solution.py:43
  60.8 6.6 fusion.104
  69.1 111.8 %all-reduce.9.cloned.1.call-done = (f32[1024,1024]{0,1:T(8,128)}, f32[32,1024]{1,0:T(8,128)}) async-done(((f32[1024,1024]{0,1:T(8,128)}, f32[32,1024]{1,0:T(8,128)}), (f32[1024,1024]{0,1:T(8,128)}, f32[32,1024]{1,0:T(8,128)})) %all-reduce.9.cloned.1.call-update) | async-done | bytes 4325392 | tf_op jit(solution)/shard_map/psum | solution.py:51
  180.9 7.6 %add_add_fusion = f32[1024,1024]{0,1:T(8,128)} fusion(f32[1024,1024]{0,1:T(8,128)} %get-tuple-element.303, f32[1024]{0:T(1024)S(1)} %bitcast.288, f32[1024]{0:T(1024)S(1)} %bitcast.281, f32[1024]{0:T(1024)S(1)} %bitcast.274), kind=kLoop, calls=%fused_computation.92 | loop fusion | flops 20971520 | bytes 8400896 | tf_op jit(solution)/shard_map/add | solution.py:52
  188.5 5.3 copy.24
  193.8 7.4 %fusion.74 = f32[1024,1024]{1,0:T(8,128)S(1)} fusion(f32[1024,1024]{1,0:T(8,128)} %copy.24, f32[1024,1024]{0,1:T(8,128)} %get-tuple-element.303, f32[1024]{0:T(1024)S(1)} %bitcast.289, f32[1024]{0:T(1024)S(1)} %bitcast.282, f32[1024]{0:T(1024)S(1)} %bitcast.275), kind=kLoop, calls=%fused_computation.90 | loop fusion | flops 23068672 | bytes 12595200 | tf_op jit(solution)/shard_map/jit(cholesky)/div | solution.py:53
  203.1 11.7 %cholesky.223 = f32[128,128]{1,0:T(8,128)S(1)} custom-call(f32[128,128]{1,0:T(8,128)S(1)} %cholesky.580), custom_call_target="Cholesky" | custom-call | tf_op jit(solution)/shard_map/jit(cholesky)/cholesky | solution.py:53
  214.9 2.5 cholesky.255
  217.4 9.8 %custom-call.64 = f32[1,128,128]{1,2,0:T(8,128)S(1)} custom-call(f32[1,128,128]{2,1,0:T(8,128)S(1)} %get-tuple-element.343), custom_call_target="InvertDiagBlocksLowerTriangular" | custom-call | tf_op jit(solution)/shard_map/jit(cholesky)/cholesky | solution.py:53
  227.2 2.4 constant_dynamic-update-slice_fusion.93
  231.1 11.7 %cholesky.244 = f32[128,128]{1,0:T(8,128)S(1)} custom-call(f32[128,128]{1,0:T(8,128)S(1)} %cholesky.584), custom_call_target="Cholesky" | custom-call | tf_op jit(solution)/shard_map/jit(cholesky)/cholesky | solution.py:53
  243.5 10.0 %custom-call.65 = f32[1,128,128]{1,2,0:T(8,128)S(1)} custom-call(f32[1,128,128]{2,1,0:T(8,128)S(1)} %get-tuple-element.340), custom_call_target="InvertDiagBlocksLowerTriangular" | custom-call | tf_op jit(solution)/shard_map/jit(cholesky)/cholesky | solution.py:53
  254.7 2.1 convolution_subtract_fusion.1
  256.9 11.7 %cholesky.468 = f32[128,128]{1,0:T(8,128)S(1)} custom-call(f32[128,128]{1,0:T(8,128)S(1)} %cholesky.589), custom_call_target="Cholesky" | custom-call | tf_op jit(solution)/shard_map/jit(cholesky)/cholesky | solution.py:53
  269.8 9.8 %custom-call.66 = f32[1,128,128]{1,2,0:T(8,128)S(1)} custom-call(f32[1,128,128]{2,1,0:T(8,128)S(1)} %get-tuple-element.337), custom_call_target="InvertDiagBlocksLowerTriangular" | custom-call | tf_op jit(solution)/shard_map/jit(cholesky)/cholesky | solution.py:53
  280.8 2.3 convolution_subtract_fusion.2
  283.1 12.1 %cholesky.487 = f32[128,128]{1,0:T(8,128)S(1)} custom-call(f32[128,128]{1,0:T(8,128)S(1)} %cholesky.594), custom_call_target="Cholesky" | custom-call | tf_op jit(solution)/shard_map/jit(cholesky)/cholesky | solution.py:53
  296.5 9.8 %custom-call.67 = f32[1,128,128]{1,2,0:T(8,128)S(1)} custom-call(f32[1,128,128]{2,1,0:T(8,128)S(1)} %get-tuple-element.334), custom_call_target="InvertDiagBlocksLowerTriangular" | custom-call | tf_op jit(solution)/shard_map/jit(cholesky)/cholesky | solution.py:53
  307.5 2.3 convolution_subtract_fusion.3
  309.8 11.7 %cholesky.506 = f32[128,128]{1,0:T(8,128)S(1)} custom-call(f32[128,128]{1,0:T(8,128)S(1)} %cholesky.599), custom_call_target="Cholesky" | custom-call | tf_op jit(solution)/shard_map/jit(cholesky)/cholesky | solution.py:53
  322.8 9.8 %custom-call.68 = f32[1,128,128]{1,2,0:T(8,128)S(1)} custom-call(f32[1,128,128]{2,1,0:T(8,128)S(1)} %get-tuple-element.331), custom_call_target="InvertDiagBlocksLowerTriangular" | custom-call | tf_op jit(solution)/shard_map/jit(cholesky)/cholesky | solution.py:53
  333.7 2.5 convolution_subtract_fusion.4
  336.1 11.7 %cholesky.526 = f32[128,128]{1,0:T(8,128)S(1)} custom-call(f32[128,128]{1,0:T(8,128)S(1)} %cholesky.604), custom_call_target="Cholesky" | custom-call | tf_op jit(solution)/shard_map/jit(cholesky)/cholesky | solution.py:53
  349.1 9.8 %custom-call.69 = f32[1,128,128]{1,2,0:T(8,128)S(1)} custom-call(f32[1,128,128]{2,1,0:T(8,128)S(1)} %get-tuple-element.328), custom_call_target="InvertDiagBlocksLowerTriangular" | custom-call | tf_op jit(solution)/shard_map/jit(cholesky)/cholesky | solution.py:53
  359.9 2.0 convolution_subtract_fusion.5
  361.9 11.7 %cholesky.546 = f32[128,128]{1,0:T(8,128)S(1)} custom-call(f32[128,128]{1,0:T(8,128)S(1)} %cholesky.609), custom_call_target="Cholesky" | custom-call | tf_op jit(solution)/shard_map/jit(cholesky)/cholesky | solution.py:53
  374.9 10.0 %custom-call.70 = f32[1,128,128]{1,2,0:T(8,128)S(1)} custom-call(f32[1,128,128]{2,1,0:T(8,128)S(1)} %get-tuple-element.325), custom_call_target="InvertDiagBlocksLowerTriangular" | custom-call | tf_op jit(solution)/shard_map/jit(cholesky)/cholesky | solution.py:53
  387.5 11.7 %cholesky.564 = f32[128,128]{1,0:T(8,128)S(1)} custom-call(f32[128,128]{1,0:T(8,128)S(1)} %convolution_subtract_fusion.6), custom_call_target="Cholesky" | custom-call | tf_op jit(solution)/shard_map/jit(cholesky)/cholesky | solution.py:53
  406.2 4.8 select_select_fusion
  411.0 23.0 %while.38 = (s32[]{:T(128)}, f32[1024,1024]{1,0:T(8,128)}, s32[8,2]{0,1:T(2,128)S(1)}, f32[8,128,128]{2,1,0:T(8,128)S(1)}, s32[]{:T(128)}) while((s32[]{:T(128)}, f32[1024,1024]{1,0:T(8,128)}, s32[8,2]{0,1:T(2,128)S(1)}, f32[8,128,128]{2,1,0:T(8,128)S(1)}, s32[]{:T(128)}) %tuple.182), condition=%wide.while_cond, body=%wide.while_body.sunk | while | flops 2 | bytes 131181 | solution.py:58
  411.6 2.3 bitcast_dynamic-update-slice_fusion.2
  414.5 2.3 bitcast_dynamic-update-slice_fusion.2
  417.3 2.3 bitcast_dynamic-update-slice_fusion.2
  420.2 2.3 bitcast_dynamic-update-slice_fusion.2
  423.1 2.3 bitcast_dynamic-update-slice_fusion.2
  426.0 2.3 bitcast_dynamic-update-slice_fusion.2
  428.9 2.3 bitcast_dynamic-update-slice_fusion.2
  431.8 2.2 bitcast_dynamic-update-slice_fusion.2
  434.0 78.8 %custom-call.74 = f32[8,128,128]{1,2,0:T(8,128)S(1)} custom-call(f32[8,128,128]{2,1,0:T(8,128)S(1)} %get-tuple-element.269), custom_call_target="InvertDiagBlocksLowerTriangular" | custom-call | tf_op jit(solution)/shard_map/jit(_cho_solve)/triangular_solve | solution.py:58
  535.3 20.4 %all_gather.15 = f32[35,2048]{1,0:T(8,128)S(1)} all-gather(f32[35,128]{1,0:T(8,128)S(1)} %pad_maximum_fusion.1), channel_id=1, replica_groups=mesh['groups'=2,'pts'=8,'lm'=2] {'pts','lm'}, dimensions={1}, use_global_device_ids=true | all-gather | bytes 304640 | tf_op jit(solution)/shard_map/all_gather | solution.py:62
  555.7 2.7 while.36
  560.2 30.1 %all-reduce.2 = (f32[32]{0:T(128)S(1)}, f32[32]{0:T(128)S(1)}) all-reduce(f32[32]{0:T(128)S(1)} %get-tuple-element.274, f32[32]{0:T(128)S(1)} %get-tuple-element.273), channel_id=1, replica_groups=mesh['groups'=2,'pts'=8,'lm'=2] {'pts','lm'}, use_global_device_ids=true, to_apply=%region_20.22 | all-reduce | flops 64 | bytes 512 | tf_op jit(solution)/shard_map/psum | solution.py:65
  590.3 55.5 %all-reduce.7.cloned.1.call-done = f32[32,1024]{1,0:T(8,128)} async-done(((f32[32,1024]{1,0:T(8,128)}), f32[32,1024]{1,0:T(8,128)}) %all-reduce.7.cloned.1.call-update) | async-done | bytes 131088 | tf_op jit(solution)/shard_map/psum | solution.py:65
  669.2 22.9 %all_gather.16 = f32[35,2048]{1,0:T(8,128)S(1)} all-gather(f32[35,128]{1,0:T(8,128)S(1)} %pad_maximum_fusion), channel_id=1, replica_groups=mesh['groups'=2,'pts'=8,'lm'=2] {'pts','lm'}, dimensions={1}, use_global_device_ids=true | all-gather | bytes 304640 | tf_op jit(solution)/shard_map/all_gather | solution.py:62
  692.0 2.7 while.37
  695.0 29.8 %all-reduce.1 = (f32[32]{0:T(128)S(1)}, f32[32]{0:T(128)S(1)}) all-reduce(f32[32]{0:T(128)S(1)} %get-tuple-element.272, f32[32]{0:T(128)S(1)} %get-tuple-element.271), channel_id=1, replica_groups=mesh['groups'=2,'pts'=8,'lm'=2] {'pts','lm'}, use_global_device_ids=true, to_apply=%region_27.29 | all-reduce | flops 64 | bytes 512 | tf_op jit(solution)/shard_map/psum | solution.py:65
  (215 shorter events, 86.4 us)
Async XLA Ops:
  7.2 173.7 %all-reduce.9.cloned.1.call-start = ((), (), s32[]{:S(2)}) async-start(), calls=%async_computation.1 | async-start | bytes 8650752 | tf_op jit(solution)/shard_map/psum | solution.py:51
  69.0 576.8 %all-reduce.7.cloned.1.call-start = ((), (), s32[]{:S(2)}) async-start(), calls=%async_computation | async-start | bytes 262144 | tf_op jit(solution)/shard_map/psum | solution.py:65
  201.2 1.9 copy-start
  406.1 106.7 %copy-start.1 = (f32[32,1024]{1,0:T(8,128)S(1)}, f32[32,1024]{1,0:T(8,128)}, u32[]{:S(2)}) copy-start(f32[32,1024]{1,0:T(8,128)} %get-tuple-element.304) | copy-start | bytes 393220
  518.5 16.7 %copy-start.2 = (f32[3,128]{1,0:T(4,128)S(1)}, f32[3,128]{1,0:T(4,128)}, u32[]{:S(2)}) copy-start(f32[3,128]{1,0:T(4,128)} %param.10) | copy-start | bytes 4612
Sparse Core Ops, SparseCore 0:
  69.1 111.6 all-reduce.8
  560.3 85.4 all-reduce.6
